TPU v7x, 32 devices: a whole 2x2x4 slice. The times are simulated.
32 devices in a mesh: ep: 4 (over z), dp: 8 (over y, x, core).
Axes of the slice: x: 2, y: 2, z: 4, core: 2. Of those that a mesh axis runs over, the one named last changes fastest.
Arguments:
- tokens: bfloat16 [16384, 256], P(('dp', 'ep'))
- dy_out: bfloat16 [16384, 256], P(('dp', 'ep'))
- dense_w1: bfloat16 [256, 256], replicated
- route_idx1: int32 [16384, 2], P(('dp', 'ep'))
- route_gate1: float32 [16384, 2], P(('dp', 'ep'))
- w_gate1: bfloat16 [8, 256, 896], P('ep')
- w_up1: bfloat16 [8, 256, 896], P('ep')
- w_down1: bfloat16 [8, 896, 256], P('ep')
- dense_w2: bfloat16 [256, 256], replicated
- route_idx2: int32 [16384, 2], P(('dp', 'ep'))
- route_gate2: float32 [16384, 2], P(('dp', 'ep'))
- w_gate2: bfloat16 [8, 256, 896], P('ep')
- w_up2: bfloat16 [8, 256, 896], P('ep')
- w_down2: bfloat16 [8, 896, 256], P('ep')
Outputs:
- output 1: bfloat16 [16384, 256], P(('dp', 'ep'))
- output 2: bfloat16 [256, 256], P(('dp', 'ep'))
- output 3: bfloat16 [8, 256, 896], P('ep', 'dp')
- output 4: bfloat16 [8, 256, 896], P('ep', 'dp')
- output 5: bfloat16 [8, 896, 256], P('ep', None, 'dp')
- output 6: bfloat16 [256, 256], P(('dp', 'ep'))
- output 7: bfloat16 [8, 256, 896], P('ep', 'dp')
- output 8: bfloat16 [8, 256, 896], P('ep', 'dp')
- output 9: bfloat16 [8, 896, 256], P('ep', None, 'dp')
All inputs are finite; a program needn't handle non-finite values.
Results may differ from a plain program's by a relative error of at most 0.02.
Values are sent between devices in bfloat16 or wider.
A program may use at most 1 GiB of HBM per device.

v0:
```python
import jax
import jax.numpy as jnp
from jax import lax
from jax.sharding import PartitionSpec as P


def copy_rows(route_idx, n_exp, capacity):
    flat_exp = route_idx.reshape(-1)
    n_copies = flat_exp.shape[0]
    order = jnp.argsort(flat_exp, stable=True).astype(jnp.int32)
    sorted_exp = jnp.take(flat_exp, order)
    counts = jnp.zeros((n_exp,), jnp.int32).at[flat_exp].add(1)
    starts = jnp.cumsum(counts, dtype=jnp.int32) - counts
    dest_row = sorted_exp * capacity + jnp.arange(n_copies, dtype=jnp.int32) - jnp.take(starts, sorted_exp)
    return jnp.zeros((n_copies,), jnp.int32).at[order].set(dest_row).reshape(route_idx.shape)


def row_fill(flat_pos, values, n_rows, empty):
    return jnp.full((n_rows,), empty, values.dtype).at[flat_pos.reshape(-1)].set(values.reshape(-1))


def dispatch(x_loc, dense_w, route_idx, n_exp):
    n_tok, top_k = route_idx.shape
    capacity = 2 * n_tok * top_k // n_exp
    mixed = (x_loc.astype(jnp.float32) + jnp.dot(x_loc, dense_w, preferred_element_type=jnp.float32)).astype(jnp.bfloat16)
    flat_pos = copy_rows(route_idx, n_exp, capacity)
    tok_ids = jnp.broadcast_to(jnp.arange(n_tok, dtype=jnp.int32)[:, None], (n_tok, top_k))
    row_tok = row_fill(flat_pos, tok_ids, n_exp * capacity, n_tok)
    send = jnp.take(mixed, row_tok, axis=0, mode='fill', fill_value=0).reshape(n_exp, capacity, -1)
    recv = lax.all_to_all(send, 'ep', 0, 1, tiled=True)
    return mixed, flat_pos, row_tok, recv


def expert_hidden(recv, w_gate, w_up):
    a_pre = jnp.einsum('ecd,edf->ecf', recv, w_gate, preferred_element_type=jnp.float32)
    b_pre = jnp.einsum('ecd,edf->ecf', recv, w_up, preferred_element_type=jnp.float32)
    hidden = (jax.nn.silu(a_pre) * b_pre).astype(jnp.bfloat16)
    return a_pre, b_pre, hidden


def combine(mixed, hidden, w_down, flat_pos, route_gate):
    expert_out = jnp.einsum('ecf,efd->ecd', hidden, w_down, preferred_element_type=jnp.float32).astype(jnp.bfloat16)
    returned = lax.all_to_all(expert_out, 'ep', 1, 0, tiled=True)
    returned = returned.reshape(-1, returned.shape[-1])
    picked = jnp.take(returned, flat_pos, axis=0)
    return (mixed.astype(jnp.float32) + jnp.sum(route_gate[:, :, None] * picked, axis=1)).astype(jnp.bfloat16)


def layer_backward(grad_y, x_loc, dense_w, route_gate, w_gate, w_up, w_down, n_exp, flat_pos, row_tok, recv, a_pre, b_pre, hidden):
    n_rows = row_tok.shape[0]
    capacity = n_rows // n_exp
    row_gate = row_fill(flat_pos, route_gate, n_rows, 0.0)
    grad_send = (jnp.take(grad_y, row_tok, axis=0, mode='fill', fill_value=0) * row_gate[:, None]).astype(jnp.bfloat16)
    grad_out = lax.all_to_all(grad_send.reshape(n_exp, capacity, -1), 'ep', 0, 1, tiled=True)
    grad_hidden = jnp.einsum('ecd,efd->ecf', grad_out, w_down, preferred_element_type=jnp.float32).astype(jnp.bfloat16)
    grad_down = jnp.einsum('ecf,ecd->efd', hidden, grad_out, preferred_element_type=jnp.float32)
    sigma_a = jax.nn.sigmoid(a_pre)
    hidden_wide = grad_hidden.astype(jnp.float32)
    grad_a = (hidden_wide * b_pre * sigma_a * (1.0 + a_pre * (1.0 - sigma_a))).astype(jnp.bfloat16)
    grad_b = (hidden_wide * a_pre * sigma_a).astype(jnp.bfloat16)
    grad_gate = jnp.einsum('ecd,ecf->edf', recv, grad_a, preferred_element_type=jnp.float32)
    grad_up = jnp.einsum('ecd,ecf->edf', recv, grad_b, preferred_element_type=jnp.float32)
    grad_recv = (jnp.einsum('ecf,edf->ecd', grad_a, w_gate, preferred_element_type=jnp.float32)
                 + jnp.einsum('ecf,edf->ecd', grad_b, w_up, preferred_element_type=jnp.float32)).astype(jnp.bfloat16)
    grad_back = lax.all_to_all(grad_recv, 'ep', 1, 0, tiled=True)
    grad_back = grad_back.reshape(-1, grad_back.shape[-1])
    grad_picked = jnp.take(grad_back, flat_pos, axis=0)
    grad_mixed = (grad_y.astype(jnp.float32) + jnp.sum(grad_picked, axis=1, dtype=jnp.float32)).astype(jnp.bfloat16)
    grad_dense = jnp.einsum('td,te->de', x_loc, grad_mixed, preferred_element_type=jnp.float32)
    grad_x = (grad_mixed.astype(jnp.float32) + jnp.einsum('te,de->td', grad_mixed, dense_w, preferred_element_type=jnp.float32)).astype(jnp.bfloat16)
    return grad_x, (grad_dense, grad_gate, grad_up, grad_down)


def reduce_grads(partials):
    grad_dense, grad_gate, grad_up, grad_down = [piece.astype(jnp.bfloat16) for piece in partials]
    return (lax.psum_scatter(grad_dense, ('dp', 'ep'), scatter_dimension=0, tiled=True),
            lax.psum_scatter(grad_gate, 'dp', scatter_dimension=1, tiled=True),
            lax.psum_scatter(grad_up, 'dp', scatter_dimension=1, tiled=True),
            lax.psum_scatter(grad_down, 'dp', scatter_dimension=2, tiled=True))


def solution(mesh):
    ep_size = mesh.shape['ep']
    tok_spec = P(('dp', 'ep'), None)
    exp_spec = P('ep', None, None)
    layer_specs = (P(None, None), tok_spec, tok_spec, exp_spec, exp_spec, exp_spec)
    grad_specs = (P(('dp', 'ep'), None), P('ep', 'dp', None), P('ep', 'dp', None), P('ep', None, 'dp'))

    def local_step(tokens, dy_out, dense_w1, route_idx1, route_gate1, w_gate1, w_up1, w_down1, dense_w2, route_idx2, route_gate2, w_gate2, w_up2, w_down2):
        n_exp = w_gate1.shape[0] * ep_size
        mixed_one, place_one, rowtok_one, recv_one = dispatch(tokens, dense_w1, route_idx1, n_exp)
        a_one, b_one, hid_one = expert_hidden(recv_one, w_gate1, w_up1)
        mid_tok = combine(mixed_one, hid_one, w_down1, place_one, route_gate1)
        mixed_two, place_two, rowtok_two, recv_two = dispatch(mid_tok, dense_w2, route_idx2, n_exp)
        a_two, b_two, hid_two = expert_hidden(recv_two, w_gate2, w_up2)
        grad_mid, parts_two = layer_backward(dy_out, mid_tok, dense_w2, route_gate2, w_gate2, w_up2, w_down2, n_exp, place_two, rowtok_two, recv_two, a_two, b_two, hid_two)
        grads_two = reduce_grads(parts_two)
        grad_tok, parts_one = layer_backward(grad_mid, tokens, dense_w1, route_gate1, w_gate1, w_up1, w_down1, n_exp, place_one, rowtok_one, recv_one, a_one, b_one, hid_one)
        grads_one = reduce_grads(parts_one)
        return (grad_tok,) + grads_one + grads_two

    return jax.shard_map(local_step, mesh=mesh, in_specs=(tok_spec, tok_spec) + layer_specs + layer_specs,
                         out_specs=(tok_spec,) + grad_specs + grad_specs, check_vma=False)
```

profile of v0, /device:TPU:0, one launch (start us, length us, event | category | flops | bytes accessed | tf_op | source)
XLA Modules:
  0.0 733.6 jit_solution(3639386982449098292)
XLA Ops:
  8.5 7.6 %scatter_custom_fusion.4 = s32[8]{0:T(128)S(1)} fusion(s32[1024]{0:T(1024)S(1)} %bitcast.124, s32[1024]{0:T(1024)S(1)} %broadcast.118, s32[]{:T(128)} %constant.42.clone.1), kind=kCustom, calls=%fused_computation.115 | custom fusion | flops 1024 | bytes 36 | tf_op jit(solution)/shard_map/scatter-add | solution.py:12
  16.9 4.4 sort.32
  21.3 4.5 gather_fusion.2
  25.8 5.2 select_subtract_fusion
  40.6 7.5 %gather_fusion.3 = bf16[2048,256]{1,0:T(8,128)(2,1)S(1)} fusion(bf16[512,256]{1,0:T(8,128)(2,1)S(1)} %fusion.12, s32[2048]{0:T(1024)S(1)} %fusion.18), kind=kCustom, calls=%fused_computation.4.clone | custom fusion | bytes 2105344 | tf_op jit(solution)/shard_map/jit(_take)/gather | solution.py:29
  49.4 6.4 all-to-all-start.1
  56.3 8.1 %scatter_custom_fusion = s32[8]{0:T(128)S(1)} fusion(s32[1024]{0:T(1024)S(1)} %bitcast.125, s32[1024]{0:T(1024)S(1)} %broadcast.118, s32[]{:T(128)} %constant.42.clone.1), kind=kCustom, calls=%fused_computation.117 | custom fusion | flops 1024 | bytes 36 | tf_op jit(solution)/shard_map/scatter-add | solution.py:12
  69.4 11.9 %all-to-all-done.1 = bf16[8,256,256]{2,1,0:T(8,128)(2,1)S(1)} async-done(((bf16[8,256,256]{2,1,0:T(8,128)(2,1)}), bf16[8,256,256]{2,1,0:T(8,128)(2,1)S(1)}, u32[]{:S(2)}, u32[]{:S(2)}) %all-to-all-start.1) | async-done | bytes 1048608 | tf_op jit(solution)/shard_map/all_to_all | solution.py:30
  83.0 4.7 multiply_convert_fusion.1
  96.6 4.5 gather_fusion
  102.2 5.1 select_subtract_fusion.1
  111.6 4.5 scatter_custom_fusion.2
  116.1 4.9 scatter_custom_fusion.3
  121.6 8.5 %gather_fusion.1 = bf16[2048,256]{1,0:T(8,128)(2,1)S(1)} fusion(bf16[512,256]{1,0:T(8,128)(2,1)S(1)} %copy-done.2, s32[2048]{0:T(1024)} %fusion.17), kind=kCustom, calls=%fused_computation.1.clone | custom fusion | bytes 2105344 | tf_op jit(solution)/shard_map/jit(_take)/gather | solution.py:53
  132.8 5.2 all-to-all-start
  151.2 7.5 %gather_fusion.5 = bf16[2048,256]{1,0:T(8,128)(2,1)S(1)} fusion(bf16[512,256]{1,0:T(8,128)(2,1)S(1)} %fusion.13, s32[2048]{0:T(1024)S(1)} %copy-done.33), kind=kCustom, calls=%fused_computation.5.clone | custom fusion | bytes 2105344 | tf_op jit(solution)/shard_map/jit(_take)/gather | solution.py:29
  172.7 18.6 %all-to-all-done.3 = bf16[8,256,256]{2,1,0:T(8,128)(2,1)S(1)} async-done(((bf16[8,256,256]{2,1,0:T(8,128)(2,1)}), bf16[8,256,256]{2,1,0:T(8,128)(2,1)S(1)}, u32[]{:S(2)}, u32[]{:S(2)}) %all-to-all-start.3) | async-done | bytes 1048608 | tf_op jit(solution)/shard_map/all_to_all | solution.py:30
  196.5 5.9 fusion.4
  212.1 8.9 %fusion.11 = bf16[2,896,256]{1,2,0:T(8,128)(2,1)} fusion(bf16[2,1024,256]{2,1,0:T(8,128)(2,1)} %bitcast.121, f32[2,1024,896]{2,1,0:T(8,128)} %copy-done.4, f32[2,1024,896]{2,1,0:T(8,128)} %get-tuple-element.70), kind=kOutput, calls=%fused_computation.43 | convolution fusion | flops 950992896 | bytes 16646144 | tf_op jit(solution)/shard_map/ecf,ecd->efd/dot_general | solution.py:56
  221.5 4.5 scatter_custom_fusion.7
  230.6 6.4 all-to-all-done.4
  242.6 5.6 convert_reduce_fusion.1
  248.5 9.0 %gather_fusion.7 = bf16[2048,256]{1,0:T(8,128)(2,1)} fusion(bf16[512,256]{1,0:T(8,128)(2,1)S(1)} %fusion.14, s32[2048]{0:T(1024)S(1)} %copy-done.32), kind=kCustom, calls=%fused_computation.6.clone | custom fusion | bytes 2105344 | tf_op jit(solution)/shard_map/jit(_take)/gather | solution.py:53
  269.8 19.7 %all-to-all-done.5 = bf16[8,256,256]{2,1,0:T(8,128)(2,1)} async-done(((bf16[8,256,256]{2,1,0:T(8,128)(2,1)}), bf16[8,256,256]{2,1,0:T(8,128)(2,1)}, u32[]{:S(2)}, u32[]{:S(2)}) %all-to-all-start.5) | async-done | bytes 1048608 | tf_op jit(solution)/shard_map/all_to_all | solution.py:54
  295.5 8.9 %fusion.9 = (bf16[2,1024,896]{2,1,0:T(8,128)(2,1)}, bf16[2,1024,896]{2,1,0:T(8,128)(2,1)S(1)}) fusion(f32[2,1024,896]{2,1,0:T(8,128)} %copy-done.3, f32[2,1024,896]{2,1,0:T(8,128)} %get-tuple-element.69, bf16[2,1024,256]{2,1,0:T(8,128)(2,1)S(1)} %bitcast.123, bf16[2,896,256]{2,1,0:T(8,128)(2,1)} %param.29), kind=kOutput, calls=%fused_computation.30 | convolution fusion | flops 967049216 | bytes 23986176 | tf_op jit(solution)/shard_map/ecd,efd->ecf/dot_general | solution.py:55
  323.2 20.8 %all-to-all-done.6 = bf16[2,1024,256]{2,0,1:T(2,128)(2,1)S(1)} async-done(((bf16[2,1024,256]{2,0,1:T(2,128)(2,1)}), bf16[2,1024,256]{2,0,1:T(2,128)(2,1)S(1)}, u32[]{:S(2)}, u32[]{:S(2)}) %all-to-all-start.6) | async-done | bytes 1048608 | tf_op jit(solution)/shard_map/all_to_all | solution.py:65
  350.6 5.6 convert_reduce_fusion
  358.3 116.2 %reduce-scatter.17.cloned.1.call-done = bf16[8,256]{1,0:T(8,128)(2,1)} async-done(((bf16[256,256]{1,0:T(8,128)(2,1)}), bf16[8,256]{1,0:T(8,128)(2,1)}) %reduce-scatter.17.cloned.1.call-update) | async-done | bytes 4112 | tf_op jit(solution)/shard_map/reduce_scatter | solution.py:76
  474.5 35.3 %reduce-scatter.15.cloned.1.call-done = bf16[2,896,32]{1,2,0:T(8,128)(2,1)} async-done(((bf16[2,896,256]{1,2,0:T(8,128)(2,1)}), bf16[2,896,32]{1,2,0:T(8,128)(2,1)}) %reduce-scatter.15.cloned.1.call-update) | async-done | bytes 114704 | tf_op jit(solution)/shard_map/reduce_scatter | solution.py:79
  509.8 39.0 %reduce-scatter.11.cloned.1.call-done = bf16[2,32,896]{2,1,0:T(8,128)(2,1)} async-done(((bf16[2,256,896]{2,1,0:T(8,128)(2,1)}), bf16[2,32,896]{2,1,0:T(8,128)(2,1)}) %reduce-scatter.11.cloned.1.call-update) | async-done | bytes 114704 | tf_op jit(solution)/shard_map/reduce_scatter | solution.py:77
  548.7 39.1 %reduce-scatter.13.cloned.1.call-done = bf16[2,32,896]{2,1,0:T(8,128)(2,1)} async-done(((bf16[2,256,896]{2,1,0:T(8,128)(2,1)}), bf16[2,32,896]{2,1,0:T(8,128)(2,1)}) %reduce-scatter.13.cloned.1.call-update) | async-done | bytes 114704 | tf_op jit(solution)/shard_map/reduce_scatter | solution.py:78
  587.9 138.4 %reduce-scatter.25.cloned.1.call-done = bf16[8,256]{1,0:T(8,128)(2,1)} async-done(((bf16[256,256]{1,0:T(8,128)(2,1)}), bf16[8,256]{1,0:T(8,128)(2,1)}) %reduce-scatter.25.cloned.1.call-update) | async-done | bytes 4112
  (206 shorter events, 135.8 us)
Async XLA Ops:
  7.2 189.3 %copy-start = (bf16[2,256,896]{2,1,0:T(8,128)(2,1)S(1)}, bf16[2,256,896]{2,1,0:T(8,128)(2,1)}, u32[]{:S(2)}) copy-start(bf16[2,256,896]{2,1,0:T(8,128)(2,1)} %param.33) | copy-start | bytes 2752516
  7.2 32.8 %copy-start.29 = (bf16[256,256]{1,0:T(8,128)(2,1)S(1)}, bf16[256,256]{1,0:T(8,128)(2,1)}, u32[]{:S(2)}) copy-start(bf16[256,256]{1,0:T(8,128)(2,1)} %param.24) | copy-start | bytes 393220
  7.2 32.8 %copy-start.21 = (bf16[512,256]{1,0:T(8,128)(2,1)S(1)}, bf16[512,256]{1,0:T(8,128)(2,1)}, u32[]{:S(2)}) copy-start(bf16[512,256]{1,0:T(8,128)(2,1)} %param.22) | copy-start | bytes 786436
  35.4 12.7 %copy-start.41 = (s32[1024]{0:T(1024)}, s32[1024]{0:T(1024)S(1)}, u32[]{:S(2)}) copy-start(s32[1024]{0:T(1024)S(1)} %compare_select_fusion.8) | copy-start | bytes 12292
  48.1 33.3 %copy-start.12 = (bf16[2,256,896]{2,1,0:T(8,128)(2,1)S(1)}, bf16[2,256,896]{2,1,0:T(8,128)(2,1)}, u32[]{:S(2)}) copy-start(bf16[2,256,896]{2,1,0:T(8,128)(2,1)} %param.27) | copy-start | bytes 2752516
  49.4 31.9 %all-to-all-start.1 = ((bf16[8,256,256]{2,1,0:T(8,128)(2,1)}), bf16[8,256,256]{2,1,0:T(8,128)(2,1)S(1)}, u32[]{:S(2)}, u32[]{:S(2)}) async-start(bf16[8,256,256]{2,1,0:T(8,128)(2,1)} %bitcast.26), calls=%async_computation.1 | async-start | bytes 2097152 | tf_op jit(solution)/shard_map/all_to_all | solution.py:30
  64.3 18.3 %copy-start.43 = (s32[8]{0:T(128)}, s32[8]{0:T(128)S(1)}, u32[]{:S(2)}) copy-start(s32[8]{0:T(128)S(1)} %scatter_custom_fusion) | copy-start | bytes 100
  92.0 9.1 %copy-start.38 = (f32[512,2]{0,1:T(2,128)S(1)}, f32[512,2]{0,1:T(2,128)}, u32[]{:S(2)}) copy-start(f32[512,2]{0,1:T(2,128)} %param.32) | copy-start | bytes 12292
  92.0 29.5 %copy-start.2 = (bf16[512,256]{1,0:T(8,128)(2,1)S(1)}, bf16[512,256]{1,0:T(8,128)(2,1)}, u32[]{:S(2)}) copy-start(bf16[512,256]{1,0:T(8,128)(2,1)} %param.23) | copy-start | bytes 786436
  92.0 40.8 %all-to-all-start.2 = ((bf16[2,1024,256]{2,0,1:T(2,128)(2,1)}), bf16[2,1024,256]{2,0,1:T(2,128)(2,1)S(1)}, u32[]{:S(2)}, u32[]{:S(2)}) async-start(bf16[2,1024,256]{2,0,1:T(2,128)(2,1)} %copy.63), calls=%async_computation.2 | async-start | bytes 2097152 | tf_op jit(solution)/shard_map/all_to_all | solution.py:43
  130.0 9.2 %copy-start.39 = (f32[512,2]{0,1:T(2,128)S(1)}, f32[512,2]{0,1:T(2,128)}, u32[]{:S(2)}) copy-start(f32[512,2]{0,1:T(2,128)} %param.26) | copy-start | bytes 12292
  132.8 29.8 %all-to-all-start = ((bf16[8,256,256]{2,1,0:T(8,128)(2,1)}), bf16[8,256,256]{2,1,0:T(8,128)(2,1)}, u32[]{:S(2)}, u32[]{:S(2)}) async-start(bf16[8,256,256]{2,1,0:T(8,128)(2,1)} %bitcast.11), calls=%async_computation | async-start | bytes 2097152 | tf_op jit(solution)/shard_map/all_to_all | solution.py:54
  141.9 9.3 %copy-start.33 = (s32[2048]{0:T(1024)S(1)}, s32[2048]{0:T(1024)}, u32[]{:S(2)}) copy-start(s32[2048]{0:T(1024)} %fusion.17) | copy-start | bytes 24580
  162.6 28.7 %all-to-all-start.3 = ((bf16[8,256,256]{2,1,0:T(8,128)(2,1)}), bf16[8,256,256]{2,1,0:T(8,128)(2,1)S(1)}, u32[]{:S(2)}, u32[]{:S(2)}) async-start(bf16[8,256,256]{2,1,0:T(8,128)(2,1)} %bitcast.33), calls=%async_computation.3 | async-start | bytes 2097152 | tf_op jit(solution)/shard_map/all_to_all | solution.py:30
  193.6 32.7 %copy-start.7 = (bf16[2,4,256,256]{3,2,1,0:T(8,128)(2,1)}, bf16[2,4,256,256]{3,2,1,0:T(8,128)(2,1)S(1)}, u32[]{:S(2)}) copy-start(bf16[2,4,256,256]{3,2,1,0:T(8,128)(2,1)S(1)} %copy.65) | copy-start | bytes 3145732
  207.6 29.4 %all-to-all-start.4 = ((bf16[2,1024,256]{2,0,1:T(2,128)(2,1)}), bf16[2,1024,256]{2,0,1:T(2,128)(2,1)}, u32[]{:S(2)}, u32[]{:S(2)}) async-start(bf16[2,1024,256]{2,0,1:T(2,128)(2,1)} %copy.66), calls=%async_computation.4 | async-start | bytes 2097152 | tf_op jit(solution)/shard_map/all_to_all | solution.py:65
  211.9 146.4 %reduce-scatter.23.cloned.1.call-start = ((), (), s32[]{:S(2)}) async-start(), calls=%async_computation.21 | async-start | bytes 1032192 | tf_op jit(solution)/shard_map/reduce_scatter | solution.py:79
  221.1 137.2 %reduce-scatter.19.cloned.1.call-start = ((), (), s32[]{:S(2)}) async-start(), calls=%async_computation.19 | async-start | bytes 1032192 | tf_op jit(solution)/shard_map/reduce_scatter | solution.py:77
  238.4 9.8 %copy-start.28 = (bf16[256,256]{1,0:T(8,128)(2,1)S(1)}, bf16[256,256]{1,0:T(8,128)(2,1)}, u32[]{:S(2)}) copy-start(bf16[256,256]{1,0:T(8,128)(2,1)} %param.30) | copy-start | bytes 393220
  238.4 10.1 %copy-start.32 = (s32[2048]{0:T(1024)S(1)}, s32[2048]{0:T(1024)}, u32[]{:S(2)}) copy-start(s32[2048]{0:T(1024)} %copy-done.31) | copy-start | bytes 24580
  260.1 29.5 %all-to-all-start.5 = ((bf16[8,256,256]{2,1,0:T(8,128)(2,1)}), bf16[8,256,256]{2,1,0:T(8,128)(2,1)}, u32[]{:S(2)}, u32[]{:S(2)}) async-start(bf16[8,256,256]{2,1,0:T(8,128)(2,1)} %bitcast.115), calls=%async_computation.5 | async-start | bytes 2097152 | tf_op jit(solution)/shard_map/all_to_all | solution.py:54
  264.3 93.9 %reduce-scatter.21.cloned.1.call-start = ((), (), s32[]{:S(2)}) async-start(), calls=%async_computation.20 | async-start | bytes 1032192 | tf_op jit(solution)/shard_map/reduce_scatter | solution.py:78
  268.7 205.8 %reduce-scatter.17.cloned.1.call-start = ((), (), s32[]{:S(2)}) async-start(), calls=%async_computation.18 | async-start | bytes 135168 | tf_op jit(solution)/shard_map/reduce_scatter | solution.py:76
  269.8 240.0 %reduce-scatter.15.cloned.1.call-start = ((), (), s32[]{:S(2)}) async-start(), calls=%async_computation.17 | async-start | bytes 1032192 | tf_op jit(solution)/shard_map/reduce_scatter | solution.py:79
  295.1 253.6 %reduce-scatter.11.cloned.1.call-start = ((), (), s32[]{:S(2)}) async-start(), calls=%async_computation.15 | async-start | bytes 1032192 | tf_op jit(solution)/shard_map/reduce_scatter | solution.py:77
  295.4 10.7 %copy-start.6 = (bf16[2,4,256,256]{3,2,1,0:T(8,128)(2,1)S(1)}, bf16[2,4,256,256]{3,2,1,0:T(8,128)(2,1)}, u32[]{:S(2)}) copy-start(bf16[2,4,256,256]{3,2,1,0:T(8,128)(2,1)} %copy-done.5) | copy-start | bytes 3145732
  315.2 28.8 %all-to-all-start.6 = ((bf16[2,1024,256]{2,0,1:T(2,128)(2,1)}), bf16[2,1024,256]{2,0,1:T(2,128)(2,1)S(1)}, u32[]{:S(2)}, u32[]{:S(2)}) async-start(bf16[2,1024,256]{2,0,1:T(2,128)(2,1)} %copy.70), calls=%async_computation.6 | async-start | bytes 2097152 | tf_op jit(solution)/shard_map/all_to_all | solution.py:65
  318.8 269.1 %reduce-scatter.13.cloned.1.call-start = ((), (), s32[]{:S(2)}) async-start(), calls=%async_computation.16 | async-start | bytes 1032192 | tf_op jit(solution)/shard_map/reduce_scatter | solution.py:78
  323.1 403.2 %reduce-scatter.25.cloned.1.call-start = ((), (), s32[]{:S(2)}) async-start(), calls=%async_computation.22 | async-start | bytes 135168
  346.4 9.8 %copy-start.22 = (bf16[512,256]{1,0:T(8,128)(2,1)S(1)}, bf16[512,256]{1,0:T(8,128)(2,1)}, u32[]{:S(2)}) copy-start(bf16[512,256]{1,0:T(8,128)(2,1)} %param.22) | copy-start | bytes 786436
  346.4 10.9 %copy-start.30 = (bf16[256,256]{1,0:T(8,128)(2,1)S(1)}, bf16[256,256]{1,0:T(8,128)(2,1)}, u32[]{:S(2)}) copy-start(bf16[256,256]{1,0:T(8,128)(2,1)} %param.24) | copy-start | bytes 393220
  346.4 379.9 %copy-start.1 = (bf16[2,256,896]{2,1,0:T(8,128)(2,1)S(1)}, bf16[2,256,896]{2,1,0:T(8,128)(2,1)}, u32[]{:S(2)}) copy-start(bf16[2,256,896]{2,1,0:T(8,128)(2,1)} %param.33) | copy-start | bytes 2752516
  (30 other events, 124.7 us)
Sparse Core Ops, SparseCore 0:
  221.2 36.6 reduce-scatter.22
  261.7 35.3 reduce-scatter.18
  300.9 35.2 reduce-scatter.20
  338.9 135.5 reduce-scatter.16
  478.1 31.6 reduce-scatter.14
  513.4 35.2 reduce-scatter.10
  552.5 35.3 reduce-scatter.12
  590.7 135.5 reduce-scatter.24
where the time goes:
time: 741 us; the launch traced here: 734 us
  waiting for transfers between devices  448 us (60%)
  local copies, waits for them, and re-layouts  109 us (15%)
  matrix products  67.7 us (9%)
  other arithmetic  62.2 us (8%)
  starting transfers between devices  31.6 us (4%)
  between operations  15.5 us (2%)
    unnamed x9, waiting for transfers between devices  139 us
    reduce_scatter x1, waiting for transfers between devices, reduce_grads(): lax.psum_scatter(grad_dense, ('dp', 'ep'), scatter_dimension=0, tiled=True)  116 us
    reduce_scatter x2, waiting for transfers between devices, reduce_grads(): lax.psum_scatter(grad_up, 'dp', scatter_dimension=1, tiled=True)  39.1 us
    reduce_scatter x2, waiting for transfers between devices, reduce_grads(): lax.psum_scatter(grad_gate, 'dp', scatter_dimension=1, tiled=True)  39 us
    reduce_scatter x2, waiting for transfers between devices, reduce_grads(): lax.psum_scatter(grad_down, 'dp', scatter_dimension=2, tiled=True)  35.3 us
    all_to_all x2, waiting for transfers between devices, dispatch(): recv = lax.all_to_all(send, 'ep', 0, 1, tiled=True)  30.5 us
    all_to_all x2, waiting for transfers between devices, layer_backward(): grad_back = lax.all_to_all(grad_recv, 'ep', 1, 0, tiled=True)  27.2 us
    all_to_all x2, waiting for transfers between devices, layer_backward(): lax.all_to_all(grad_send.reshape(n_exp, capacity, -1), 'ep', 0, 1, tiled=...  21.7 us
  transfers between devices with their start and end apart: 15, of which 11 were waited for; matrix products, arithmetic and copies ran while one was open for 23% of the time, Pallas kernels for 0%

commit v1 on v0

v1 whole, which is shorter than its diff:
```python
import functools

import jax
import jax.numpy as jnp
from jax import lax
from jax.experimental import pallas as pl
from jax.experimental.pallas import tpu as pltpu
from jax.sharding import PartitionSpec as P

MESH = pl.DeviceIdType.MESH
F32, BF16 = jnp.float32, jnp.bfloat16
N_EP = 4
N_EXP = 8
CAP = 256


def nn(a, b):
    return lax.dot_general(a, b, (((1,), (0,)), ((), ())), preferred_element_type=F32)


def nt(a, b):
    return lax.dot_general(a, b, (((1,), (1,)), ((), ())), preferred_element_type=F32)


def tn(a, b):
    return lax.dot_general(a, b, (((0,), (0,)), ((), ())), preferred_element_type=F32)


def kernel(n_dp, x_ref, dy_ref, dense1, dense2, idx1, gate1, idx2, gate2, aux_ref,
           wg1_hbm, wu1_hbm, wd1_hbm, wg2_hbm, wu2_hbm, wd2_hbm,
           dx_ref, gd1_ref, ge1_ref, gd2_ref, ge2_ref,
           w_gate, w_up, w_down, auxb, posr, gater, posc, gatec, tri, ag, ret, rows_in, t_a, t_b, t_gh, hid, g_a, g_b, g_out,
           acc, mid, g_mid, gs, gr, g2, d_send, d_a, d_bs, d_b,
           w_sem, aux_send, aux_recv, ag_right, ag_left, ag_recv, ret_send, ret_recv, pair_send, pair_recv,
           plane_send, plane_recv, da_send, da_recv, db_send, db_recv):
    z = lax.axis_index('ep')
    dp = lax.axis_index('dp')
    n_chip = n_dp // 2
    core = dp % 2
    chip = dp // 2
    n_tok, d_model = x_ref.shape
    d_ff = t_a.shape[1]
    piece = d_model // n_dp

    def order(k):
        near_low = jnp.where(z == 1, jnp.where(k == 0, 1, jnp.where(k == 1, 0, k)), k)
        near_high = 3 - jnp.where(z == 2, jnp.where(k == 0, 1, jnp.where(k == 1, 0, k)), k)
        return jnp.where(z < 2, near_low, near_high)

    barrier = pltpu.get_barrier_semaphore()
    for k in range(1, N_EP):
        pl.semaphore_signal(barrier, inc=1, device_id={'ep': (z + k) % N_EP, 'dp': dp}, device_id_type=MESH)
    for k in range(1, n_dp):
        pl.semaphore_signal(barrier, inc=1, device_id={'ep': z, 'dp': (dp + k) % n_dp}, device_id_type=MESH)

    w_copies = []
    for n, (hbm, dst) in enumerate(((wg1_hbm, w_gate.at[0]), (wu1_hbm, w_up.at[0]), (wd1_hbm, w_down.at[0]),
                                    (wg2_hbm, w_gate.at[1]), (wu2_hbm, w_up.at[1]), (wd2_hbm, w_down.at[1]))):
        w_copies.append(pltpu.make_async_copy(hbm, dst, w_sem.at[n]))
        w_copies[-1].start()

    x = x_ref[...]
    ag[0, z] = (x.astype(F32) + nn(x, dense1[...])).astype(BF16)
    ag[2, z] = dy_ref[...]
    auxb[z] = aux_ref[...]

    pl.semaphore_wait(barrier, N_EP - 1 + n_dp - 1)

    def col_copy(src, dst, send, recv, to):
        return pltpu.make_async_remote_copy(src_ref=src, dst_ref=dst, send_sem=send, recv_sem=recv,
                                            device_id={'ep': to, 'dp': dp}, device_id_type=MESH)

    def row_copy(src, dst, send, recv, to):
        return pltpu.make_async_remote_copy(src_ref=src, dst_ref=dst, send_sem=send, recv_sem=recv,
                                            device_id={'ep': z, 'dp': to}, device_id_type=MESH)

    def aux_copy(k):
        return col_copy(aux_ref, auxb.at[z], aux_send.at[k], aux_recv.at[z], (z + k) % N_EP)

    for k in range(1, N_EP):
        aux_copy(k).start()

    def ag_to_right(n, s):
        return col_copy(ag.at[n, s], ag.at[n, s], ag_right.at[n, s], ag_recv.at[n, s], jnp.minimum(z + 1, N_EP - 1))

    def ag_to_left(n, s):
        return col_copy(ag.at[n, s], ag.at[n, s], ag_left.at[n, s], ag_recv.at[n, s], jnp.maximum(z - 1, 0))

    def ag_pass(n, s):
        @pl.when(jnp.logical_and(s <= z, z < N_EP - 1))
        def _():
            ag_to_right(n, s).start()

        @pl.when(jnp.logical_and(s >= z, z > 0))
        def _():
            ag_to_left(n, s).start()

    def ag_take(n, s):
        ag_to_right(n, s).wait_recv()
        ag_pass(n, s)

    def ag_step(n, k):
        inner = jnp.logical_or(z == 1, z == 2)
        outer = jnp.logical_not(inner)

        @pl.when(k == 1)
        def _():
            ag_take(n, order(1))

        @pl.when(jnp.logical_or(jnp.logical_and(k == 1, inner), jnp.logical_and(k == 2, outer)))
        def _():
            ag_take(n, order(2))

        @pl.when(k == 3)
        def _():
            ag_take(n, order(3))

    def ag_drain(n):
        def body(s, carry):
            @pl.when(jnp.logical_and(s <= z, z < N_EP - 1))
            def _():
                ag_to_right(n, s).wait_send()

            @pl.when(jnp.logical_and(s >= z, z > 0))
            def _():
                ag_to_left(n, s).wait_send()
            return carry
        lax.fori_loop(0, N_EP, body, 0)

    def ret_copy(n, s):
        return col_copy(ret.at[n, 0, s], ret.at[n, 1, z], ret_send.at[n, s], ret_recv.at[n, z], s)

    def ret_wait(n, s):
        col_copy(ret.at[n, 0, s], ret.at[n, 1, s], ret_send.at[n, s], ret_recv.at[n, s], s).wait_recv()

    def ret_drain(n):
        for k in range(1, N_EP):
            ret_copy(n, (z + k) % N_EP).wait_send()

    ag_pass(0, z)

    r_io = lax.broadcasted_iota(jnp.int32, (n_tok, n_tok), 0)
    c_io = lax.broadcasted_iota(jnp.int32, (n_tok, n_tok), 1)
    tri[...] = (c_io < r_io).astype(F32).astype(BF16)
    lane = lax.broadcasted_iota(jnp.int32, (n_tok, N_EXP), 1)
    for layer, (idx, gate) in enumerate(((idx1, gate1), (idx2, gate2))):
        hit0 = idx[:, 0:1] == lane
        hit1 = idx[:, 1:2] == lane
        hit = jnp.logical_or(hit0, hit1)
        rank = nn(tri[...], hit.astype(F32).astype(BF16))
        posc[layer] = jnp.where(hit, rank, -1.0)
        gatec[layer] = jnp.where(hit0, gate[:, 0:1], 0.0) + jnp.where(hit1, gate[:, 1:2], 0.0)
    for k in range(1, N_EP):
        s = (z + k) % N_EP
        col_copy(aux_ref, auxb.at[s], aux_send.at[k], aux_recv.at[s], s).wait_recv()
    hits = []
    for layer in range(2):
        for s in range(N_EP):
            for e in range(2):
                a = auxb[s]
                expert = (z * 2 + e).astype(F32)
                hit0 = a[4 * layer:4 * layer + 1] == expert
                hit1 = a[4 * layer + 1:4 * layer + 2] == expert
                hits.append(jnp.logical_or(hit0, hit1).astype(F32))
                gater[(layer * N_EP + s) * 2 + e] = (jnp.where(hit0, a[4 * layer + 2:4 * layer + 3], 0.0)
                                                     + jnp.where(hit1, a[4 * layer + 3:4 * layer + 4], 0.0))
    stack = jnp.concatenate(hits, axis=0)
    ranks = jnp.where(stack > 0.5, nt(stack.astype(BF16), tri[...]), -1.0)
    for n in range(4 * N_EP):
        posr[n] = ranks[n:n + 1]

    for copy in w_copies:
        copy.wait()

    slot = lax.broadcasted_iota(jnp.int32, (CAP, n_tok), 0).astype(F32)
    slot_lane = lax.broadcasted_iota(jnp.int32, (n_tok, CAP), 1).astype(F32)

    def select(layer, s, e):
        return (posr[(layer * N_EP + s) * 2 + e] == slot)

    def up_project(layer, s, e):
        rows = rows_in[layer, e, s]
        t_a[...] = nn(rows, w_gate[layer, e])
        t_b[...] = nn(rows, w_up[layer, e])

    def take_rows(layer, s, e, n):
        pick = select(layer, s, e).astype(F32).astype(BF16)
        rows_in[layer, e, s] = nn(pick, ag[n, s]).astype(BF16)

    def forward(s, e):
        take_rows(0, s, e, 0)
        up_project(0, s, e)

        def body(i, carry):
            r = pl.ds(i * 32, 32)
            a = t_a[r, :]
            hid[e, s, r, :] = (a * jax.nn.sigmoid(a) * t_b[r, :]).astype(BF16)
            return carry
        lax.fori_loop(0, CAP // 32, body, 0)
        out = nn(hid[e, s], w_down[0, e]).astype(BF16)
        ret[0, jnp.where(s == z, 1, 0), s, e] = out

    def backward(layer, s, e, n_dy, n_ret):
        up_project(layer, s, e)
        pick = select(layer, s, e)
        gate = jnp.sum(jnp.where(pick, gater[(layer * N_EP + s) * 2 + e], 0.0), axis=1, keepdims=True)
        g_out[e, s] = (nn(pick.astype(F32).astype(BF16), ag[n_dy, s]) * gate).astype(BF16)
        t_gh[...] = nt(g_out[e, s], w_down[layer, e]).astype(BF16)

        def body(i, carry):
            r = pl.ds(i * 32, 32)
            a = t_a[r, :]
            b = t_b[r, :]
            gh = t_gh[r, :].astype(F32)
            sig = jax.nn.sigmoid(a)
            hid[e, s, r, :] = (a * sig * b).astype(BF16)
            g_a[e, s, r, :] = (gh * b * sig * (1.0 + a * (1.0 - sig))).astype(BF16)
            g_b[e, s, r, :] = (gh * a * sig).astype(BF16)
            return carry
        lax.fori_loop(0, CAP // 32, body, 0)
        ret[n_ret, jnp.where(s == z, 1, 0), s, e] = (nt(g_a[e, s], w_gate[layer, e])
                                                     + nt(g_b[e, s], w_up[layer, e])).astype(BF16)

    def send_back(n, s):
        @pl.when(s != z)
        def _():
            ret_copy(n, s).start()

    def gather_back(n, layer, weighted):
        acc[...] = jnp.zeros_like(acc)

        def body(k, carry):
            s = order(k)

            @pl.when(k > 0)
            def _():
                ret_wait(n, s)

            for e in range(2):
                here = lane == s * 2 + e
                pos = jnp.sum(jnp.where(here, posc[layer], 0.0), axis=1, keepdims=True)
                got = nn((pos == slot_lane).astype(F32).astype(BF16), ret[n, 1, s, e])
                if weighted:
                    got = got * jnp.sum(jnp.where(here, gatec[layer], 0.0), axis=1, keepdims=True)
                acc[...] += got
            return carry
        lax.fori_loop(0, N_EP, body, 0)

    def weight_grads(layer):
        def body(e, carry):
            rows = rows_in[layer, e].reshape(N_EP * CAP, d_model)
            outs = g_out[e].reshape(N_EP * CAP, d_model)
            for q, (left, right) in enumerate(((rows, g_a), (rows, g_b), (outs, hid))):
                grad = tn(left, right[e].reshape(N_EP * CAP, d_ff)).astype(BF16)
                for p in range(n_dp):
                    gs[p % 2, p // 2, q * 2 + e] = grad[p * piece:(p + 1) * piece]
            return carry
        lax.fori_loop(0, 2, body, 0)

    def pair_copy(layer):
        return row_copy(gs.at[1 - core], gr.at[layer], pair_send.at[layer], pair_recv.at[layer], chip * 2 + 1 - core)

    def plane_copy(layer, k):
        to = (chip + k) % n_chip
        return row_copy(gr.at[layer, to], g2.at[layer, chip], plane_send.at[layer, k], plane_recv.at[layer, chip], to * 2 + core)

    def pair_sum(layer):
        pair_copy(layer).wait()

        def body(i, carry):
            c = i // 6
            j = i % 6
            gr[layer, c, j] = (gr[layer, c, j].astype(F32) + gs[core, c, j].astype(F32)).astype(BF16)
            return carry
        lax.fori_loop(0, n_chip * 6, body, 0)
        for k in range(1, n_chip):
            plane_copy(layer, k).start()

    def plane_sum(layer, out_ref):
        for k in range(1, n_chip):
            frm = (chip + k) % n_chip
            row_copy(gr.at[layer, frm], g2.at[layer, frm], plane_send.at[layer, k], plane_recv.at[layer, frm], frm * 2 + core).wait_recv()

        def body(j, carry):
            total = gr[layer, chip, j].astype(F32)
            for k in range(1, n_chip):
                total += g2[layer, (chip + k) % n_chip, j].astype(F32)
            out_ref[j] = total.astype(BF16)
            return carry
        lax.fori_loop(0, 6, body, 0)
        for k in range(1, n_chip):
            plane_copy(layer, k).wait_send()

    def da_copy(layer, k):
        to = (dp + k) % n_dp
        return row_copy(d_send.at[layer, to], d_a.at[layer, dp], da_send.at[layer, k], da_recv.at[layer, dp], to)

    def db_copy(layer, k):
        to = (z + k) % N_EP
        return col_copy(d_bs.at[layer, to], d_b.at[layer, z], db_send.at[layer, k], db_recv.at[layer, z], to)

    def dense_start(layer, grad):
        for p in range(n_dp):
            d_send[layer, p] = grad[p * piece:(p + 1) * piece].astype(BF16)
        for k in range(1, n_dp):
            da_copy(layer, k).start()

    def dense_middle(layer):
        for k in range(1, n_dp):
            frm = (dp + k) % n_dp
            row_copy(d_send.at[layer, frm], d_a.at[layer, frm], da_send.at[layer, k], da_recv.at[layer, frm], frm).wait_recv()
        total = d_send[layer, dp].astype(F32)
        for k in range(1, n_dp):
            total += d_a[layer, (dp + k) % n_dp].astype(F32)
        sub = piece // N_EP
        for p in range(N_EP):
            d_bs[layer, p] = total[p * sub:(p + 1) * sub].astype(BF16)
        for k in range(1, N_EP):
            db_copy(layer, k).start()

    def dense_end(layer, out_ref):
        for k in range(1, N_EP):
            frm = (z + k) % N_EP
            col_copy(d_bs.at[layer, frm], d_b.at[layer, frm], db_send.at[layer, k], db_recv.at[layer, frm], frm).wait_recv()
        total = d_bs[layer, z].astype(F32)
        for k in range(1, N_EP):
            total += d_b[layer, (z + k) % N_EP].astype(F32)
        out_ref[...] = total.astype(BF16)
        for k in range(1, n_dp):
            da_copy(layer, k).wait_send()
        for k in range(1, N_EP):
            db_copy(layer, k).wait_send()

    def forward_step(k, carry):
        s = order(k)
        ag_step(0, k)

        def experts(e, c):
            forward(s, e)
            return c
        lax.fori_loop(0, 2, experts, 0)
        send_back(0, s)
        return carry
    lax.fori_loop(0, N_EP, forward_step, 0)
    ag_pass(2, z)
    gather_back(0, 0, True)
    y = (ag[0, z].astype(F32) + acc[...]).astype(BF16)
    mid[...] = y
    ag[1, z] = (y.astype(F32) + nn(y, dense2[...])).astype(BF16)
    ag_pass(1, z)

    def second_step(k, carry):
        s = order(k)
        ag_step(2, k)
        ag_step(1, k)

        def experts(e, c):
            take_rows(1, s, e, 1)
            backward(1, s, e, 2, 1)
            return c
        lax.fori_loop(0, 2, experts, 0)
        send_back(1, s)
        return carry
    lax.fori_loop(0, N_EP, second_step, 0)
    weight_grads(1)
    pair_copy(1).start()
    gather_back(1, 1, False)
    gm = (dy_ref[...].astype(F32) + acc[...]).astype(BF16)
    gx = (gm.astype(F32) + nt(gm, dense2[...])).astype(BF16)
    g_mid[...] = gx
    ag[3, z] = gx
    ag_pass(3, z)
    dense_start(1, tn(mid[...], gm))
    pair_sum(1)

    def first_step(k, carry):
        s = order(k)
        ag_step(3, k)

        def experts(e, c):
            backward(0, s, e, 3, 2)
            return c
        lax.fori_loop(0, 2, experts, 0)
        send_back(2, s)
        return carry
    lax.fori_loop(0, N_EP, first_step, 0)
    weight_grads(0)
    pair_copy(0).start()
    dense_middle(1)
    pair_sum(0)
    gather_back(2, 0, False)
    gm1 = (g_mid[...].astype(F32) + acc[...]).astype(BF16)
    dense_start(0, tn(x_ref[...], gm1))
    dx_ref[...] = (gm1.astype(F32) + nt(gm1, dense1[...])).astype(BF16)
    plane_sum(1, ge2_ref)
    dense_middle(0)
    plane_sum(0, ge1_ref)
    dense_end(1, gd2_ref)
    dense_end(0, gd1_ref)
    for n in range(4):
        ag_drain(n)
    for n in range(3):
        ret_drain(n)
    for k in range(1, N_EP):
        aux_copy(k).wait_send()


def solution(mesh):
    n_dp = mesh.shape['dp']
    n_chip = n_dp // 2
    tok_spec = P(('dp', 'ep'), None)
    exp_spec = P('ep', None, None)
    layer_specs = (P(None, None), tok_spec, tok_spec, exp_spec, exp_spec, exp_spec)
    grad_specs = (P(('dp', 'ep'), None), P('ep', 'dp', None), P('ep', 'dp', None), P('ep', None, 'dp'))

    def local_step(tokens, dy_out, dense_w1, idx1, gate1, wg1, wu1, wd1, dense_w2, idx2, gate2, wg2, wu2, wd2):
        n_tok, d_model = tokens.shape
        d_ff = wg1.shape[2]
        piece = d_model // n_dp
        sub = piece // N_EP
        aux = jnp.concatenate([idx1.astype(F32), gate1, idx2.astype(F32), gate2], axis=1).T
        vmem = pl.BlockSpec(memory_space=pltpu.VMEM)
        hbm = pl.BlockSpec(memory_space=pl.ANY)
        dma = pltpu.SemaphoreType.DMA
        outs = pl.pallas_call(
            functools.partial(kernel, n_dp),
            out_shape=(jax.ShapeDtypeStruct((n_tok, d_model), BF16),
                       jax.ShapeDtypeStruct((sub, d_model), BF16), jax.ShapeDtypeStruct((6, piece, d_ff), BF16),
                       jax.ShapeDtypeStruct((sub, d_model), BF16), jax.ShapeDtypeStruct((6, piece, d_ff), BF16)),
            in_specs=[vmem] * 9 + [hbm] * 6,
            out_specs=[vmem] * 5,
            scratch_shapes=[
                pltpu.VMEM((2, 2, d_model, d_ff), BF16), pltpu.VMEM((2, 2, d_model, d_ff), BF16), pltpu.VMEM((2, 2, d_ff, d_model), BF16),
                pltpu.VMEM((N_EP, 8, n_tok), F32), pltpu.VMEM((4 * N_EP, 1, n_tok), F32), pltpu.VMEM((4 * N_EP, 1, n_tok), F32),
                pltpu.VMEM((2, n_tok, N_EXP), F32), pltpu.VMEM((2, n_tok, N_EXP), F32), pltpu.VMEM((n_tok, n_tok), BF16),
                pltpu.VMEM((4, N_EP, n_tok, d_model), BF16), pltpu.VMEM((3, 2, N_EP, 2, CAP, d_model), BF16),
                pltpu.VMEM((2, 2, N_EP, CAP, d_model), BF16), pltpu.VMEM((CAP, d_ff), F32), pltpu.VMEM((CAP, d_ff), F32),
                pltpu.VMEM((CAP, d_ff), BF16), pltpu.VMEM((2, N_EP, CAP, d_ff), BF16), pltpu.VMEM((2, N_EP, CAP, d_ff), BF16),
                pltpu.VMEM((2, N_EP, CAP, d_ff), BF16), pltpu.VMEM((2, N_EP, CAP, d_model), BF16),
                pltpu.VMEM((n_tok, d_model), F32), pltpu.VMEM((n_tok, d_model), BF16), pltpu.VMEM((n_tok, d_model), BF16),
                pltpu.VMEM((2, n_chip, 6, piece, d_ff), BF16), pltpu.VMEM((2, n_chip, 6, piece, d_ff), BF16),
                pltpu.VMEM((2, n_chip, 6, piece, d_ff), BF16),
                pltpu.VMEM((2, n_dp, piece, d_model), BF16), pltpu.VMEM((2, n_dp, piece, d_model), BF16),
                pltpu.VMEM((2, N_EP, sub, d_model), BF16), pltpu.VMEM((2, N_EP, sub, d_model), BF16),
                dma((6,)), dma((N_EP,)), dma((N_EP,)), dma((4, N_EP)), dma((4, N_EP)), dma((4, N_EP)), dma((3, N_EP)), dma((3, N_EP)),
                dma((2,)), dma((2,)), dma((2, n_chip)), dma((2, n_chip)), dma((2, n_dp)), dma((2, n_dp)), dma((2, N_EP)), dma((2, N_EP)),
            ],
            compiler_params=pltpu.CompilerParams(collective_id=0, has_side_effects=True, vmem_limit_bytes=67043328),
        )(tokens, dy_out, dense_w1, dense_w2, idx1, gate1, idx2, gate2, aux, wg1, wu1, wd1, wg2, wu2, wd2)
        grad_tok, gd1, ge1, gd2, ge2 = outs
        res = [grad_tok]
        for gd, ge in ((gd1, ge1), (gd2, ge2)):
            res += [gd, ge[0:2], ge[2:4], jnp.swapaxes(ge[4:6], 1, 2)]
        return tuple(res)

    return jax.shard_map(local_step, mesh=mesh, in_specs=(tok_spec, tok_spec) + layer_specs + layer_specs,
                         out_specs=(tok_spec,) + grad_specs + grad_specs, check_vma=False)
```

time: 741 us -> 172 us (0.23)
  waiting for transfers between devices: 448 us -> 0 us
  Pallas kernels: 0 us -> 161 us
  local copies, waits for them, and re-layouts: 109 us -> 8.25 us
  matrix products: 67.7 us -> 0 us
  other arithmetic: 62.2 us -> 1.32 us
  starting transfers between devices: 31.6 us -> 0 us
  between operations: 15.5 us -> 0.69 us
    reduce_scatter x7 -> x0, waiting for transfers between devices: 230 us -> none  [the longest x1 116 us: reduce_grads(): lax.psum_scatter(grad_dense, ('dp', 'ep'), scatter_dimension=0, tiled=True)]
    pallas_call x0 -> x1, Pallas kernels: none -> 161 us  [local_step(): pl.pallas_call(functools.partial(kernel, n_dp), out_shape=(jax.ShapeDtype...]
    unnamed x9 -> x0, waiting for transfers between devices: 139 us -> none
    all_to_all x7 -> x0, waiting for transfers between devices: 79.4 us -> none  [the longest x2 30.5 us: dispatch(): recv = lax.all_to_all(send, 'ep', 0, 1, tiled=True)]
    dot_general x23 -> x0, matrix products: 67.7 us -> none  [the longest x2 13.2 us: layer_backward(): jnp.einsum('ecf,ecd->efd', hidden, grad_out, preferred_element_type=jnp.f...]
    gather x14 -> x0, local copies, waits for them, and re-layouts: 56 us -> none  [the longest x2 17.4 us: layer_backward(): jnp.take(grad_y, row_tok, axis=0, mode='fill', fill_value=0)]
    all_to_all x7 -> x0, starting transfers between devices: 30.8 us -> none  [the longest x2 9.89 us: dispatch(): recv = lax.all_to_all(send, 'ep', 0, 1, tiled=True)]
    scatter x6 -> x0, local copies, waits for them, and re-layouts: 26.8 us -> none  [the longest x4 18.1 us: row_fill(): jnp.full((n_rows,), empty, values.dtype).at[flat_pos.reshape(-1)]]
  transfers between devices with their start and end apart: 15 -> 0, of which waited for: 11 -> 0; matrix products, arithmetic and copies ran while one was open for 23% -> 0% of each run, Pallas kernels for 0% -> 0%
where the time goes in v1:
time: 172 us; the launch traced here: 171 us
  Pallas kernels  161 us (94%)
  local copies, waits for them, and re-layouts  8.25 us (5%)
    pallas_call x1, Pallas kernels, local_step(): pl.pallas_call(functools.partial(kernel, n_dp), out_shape=(jax.ShapeDtype...  161 us
    unnamed x21, local copies, waits for them, and re-layouts  6.19 us

profile of v1, /device:TPU:0, one launch (start us, length us, event | category | flops | bytes accessed | tf_op | source)
XLA Modules:
  0.0 171.4 jit_solution(7546303380285736641)
XLA Ops:
  0.6 0.0 copy-start.2
  0.7 0.7 convert_element_type.6
  1.3 0.0 copy-done.2
  1.4 0.0 copy-start.3
  1.4 0.0 copy-start.4
  1.4 0.7 copy-done.3
  2.0 0.0 copy-done.4
  2.1 0.0 copy-start.1
  2.1 0.6 maximum_bitcast_fusion.aux_ref
  2.7 0.1 copy-done.1
  2.7 0.9 copy.23.idx1
  3.6 0.9 copy.24.gate1
  4.5 0.9 copy.25.idx2
  5.3 0.9 copy.26.gate2
  6.2 161.1 %shard_map.205 = (bf16[512,256]{1,0:T(8,128)(2,1)}, bf16[8,256]{1,0:T(8,128)(2,1)}, bf16[6,32,896]{2,1,0:T(8,128)(2,1)}, bf16[8,256]{1,0:T(8,128)(2,1)}, bf16[6,32,896]{2,1,0:T(8,128)(2,1)}) custom-call(bf16[512,256]{1,0:T(8,128)(2,1)} %x_ref.1, bf16[512,256]{1,0:T(8,128)(2,1)} %dy_ref.1, bf16[256,256]{1,0:T(8,128)(2,1)} %dense1.1, bf16[256,256]{1,0:T(8,128)(2,1)} %dense2.1, ...), custom_call_target="tpu_custom_call" | custom-call | tf_op jit(solution)/shard_map/pallas_call | solution.py:425
  167.3 0.0 copy-start
  167.3 2.1 %slice_bitcast_fusion = (bf16[2,896,32]{1,2,0:T(8,128)(2,1)}, bf16[2,32,896]{2,1,0:T(8,128)(2,1)}, bf16[2,32,896]{2,1,0:T(8,128)(2,1)}, bf16[2,32,896]{2,1,0:T(8...) fusion(bf16[6,32,896]{2,1,0:T(8,128)(2,1)} %get-tuple-element.18, bf16[6,32,896]{2,1,0:T(8,128)(2,1)} %get-tuple-element.16), kind=kLoop, calls=%fused_computation | loop fusion | bytes 1376256 | tf_op jit(solution)/shard_map/transpose | solution.py:453
  169.4 0.0 copy-done
  169.4 0.0 copy-start.6
  169.4 0.7 copy.30
  170.1 0.0 copy-done.6
  170.1 0.0 copy-start.5
  170.1 0.6 copy.31
  170.7 0.1 copy-done.5
  170.8 0.6 copy.32
  (1 shorter events, 0.0 us)
Async XLA Ops:
  0.6 0.7 copy-start.2
  1.4 0.7 copy-start.3
  1.4 0.7 copy-start.4
  2.1 0.7 copy-start.1
  167.3 2.1 %copy-start = (bf16[512,256]{1,0:T(8,128)(2,1)S(1)}, bf16[512,256]{1,0:T(8,128)(2,1)}, u32[]{:S(2)}) copy-start(bf16[512,256]{1,0:T(8,128)(2,1)} %get-tuple-element.37) | copy-start | bytes 786436
  169.4 0.7 copy-start.6
  170.1 0.7 copy-start.5
